TPU v7x, 32 devices: a whole 2x2x4 slice. The times are simulated.
32 devices in a mesh: grp: 4 (over x, core), sub: 8 (over z, y).
Axes of the slice: x: 2, y: 2, z: 4, core: 2. Of those that a mesh axis runs over, the one named last changes fastest.
Arguments:
- fine_res: float32 [3, 131072], P(None, ('grp', 'sub'))
- node_map: int32 [2, 131072], P(None, ('grp', 'sub')), may hold values from 0 to 16383, as said below
- connect: int32 [4, 32768], P(None, 'sub'), may hold values from 0 to 16383, as said below
- grads: float32 [3, 3, 32768], P(None, None, 'sub'), may hold values from -6 to 6
- moduli: float32 [2, 32768], P(None, 'sub'), may hold values from 0.2 to 2
- mass: float32 [16384], P('sub'), may hold values from 0.5 to 4
Outputs:
- correction: float32 [3, 131072], P(None, ('grp', 'sub'))
Inputs may be any that keep to these rules, and one draw needn't show every extreme that they name: `node_map`: fine nodes 4096 * b to 4096 * (b + 1) - 1 lie in column c = b % 8; both their entries are coarse nodes c * 2048 to (c + 1) * 2048 - 1 or the first 1024 nodes of column c + 1; the two entries are equal at vertices. `connect`: tetrahedra c * 4096 to (c + 1) * 4096 - 1 lie in column c; their nodes are coarse nodes of column c or the first 1024 nodes of column c + 1.
All inputs are finite; a program needn't handle non-finite values.
Results may differ from a plain program's by a relative error of at most 0.0001.
Values sent between devices are 32-bit elements; how exact they have to be, the bound alone decides.
A program may use at most 64 MiB of HBM per device.

v0:
```python
import functools

import jax
import jax.numpy as jnp
from jax import lax
from jax.experimental import pallas as pl
from jax.experimental.pallas import tpu as pltpu
from jax.sharding import PartitionSpec as P

CI = 1024
ITERS = 3
LANES = 128
TILE = 512
F32 = jnp.float32
BF16 = jnp.bfloat16
NT = (((1,), (1,)), ((), ()))


def split(value):
    high = value.astype(BF16)
    return high, (value - high.astype(F32)).astype(BF16)


def hots(index, rows):
    lane = index & (LANES - 1)
    row = index // LANES
    width = index.shape[1]
    lane_hot = jnp.where(lax.broadcasted_iota(jnp.int32, (LANES, width), 0) == lane, 1.0, 0.0).astype(BF16)
    row_hot = lax.broadcasted_iota(jnp.int32, (rows, width), 0) == row
    return lane_hot, row_hot


def pick(parts, lane_hot, row_hot, rows):
    got = jnp.dot(parts, lane_hot, preferred_element_type=F32)
    half = 3 * rows
    got = got[:half] + got[half:]
    return [
        jnp.sum(jnp.where(row_hot, got[d * rows : (d + 1) * rows], 0.0), axis=0, keepdims=True)
        for d in range(3)
    ]


def spread(values, lane_hot, row_hot):
    placed = []
    for value in values:
        placed.append(jnp.where(row_hot, value, 0.0))
    placed = jnp.concatenate(placed, axis=0)
    parts = jnp.concatenate(split(placed), axis=0)
    got = lax.dot_general(parts, lane_hot, NT, preferred_element_type=F32)
    half = got.shape[0] // 2
    return got[:half] + got[half:]


def field_parts(field_ref, rows):
    field = field_ref[...].reshape(3 * rows, LANES)
    return jnp.concatenate(split(field), axis=0)


def restrict_kernel(fine_ref, map_ref, out_ref, *, rows, nodes):
    base = lax.axis_index("sub") * nodes
    total = jnp.zeros((3 * rows, LANES), F32)
    for at in range(0, fine_ref.shape[1], TILE):
        values = [0.5 * fine_ref[d : d + 1, at : at + TILE] for d in range(3)]
        for k in range(2):
            lane_hot, row_hot = hots(map_ref[k : k + 1, at : at + TILE] - base, rows)
            total = total + spread(values, lane_hot, row_hot)
    out_ref[...] = total.reshape(3, rows, LANES)


def prolong_kernel(field_ref, map_ref, out_ref, *, rows, nodes):
    base = lax.axis_index("sub") * nodes
    parts = field_parts(field_ref, rows)
    for at in range(0, out_ref.shape[1], TILE):
        both = []
        for k in range(2):
            lane_hot, row_hot = hots(map_ref[k : k + 1, at : at + TILE] - base, rows)
            both.append(pick(parts, lane_hot, row_hot, rows))
        for d in range(3):
            out_ref[d : d + 1, at : at + TILE] = 0.5 * (both[0][d] + both[1][d])


def force_kernel(field_ref, conn_ref, grads_ref, moduli_ref, out_ref, *, rows, nodes):
    base = lax.axis_index("sub") * nodes
    parts = field_parts(field_ref, rows)
    total = jnp.zeros((3 * rows, LANES), F32)
    for at in range(0, conn_ref.shape[1], TILE):
        cut = slice(at, at + TILE)
        grad = [[grads_ref[i, a : a + 1, cut] for i in range(3)] for a in range(3)]
        grad.append([-(grad[0][i] + grad[1][i] + grad[2][i]) for i in range(3)])
        first = moduli_ref[0:1, cut]
        second = moduli_ref[1:2, cut]
        hot = [hots(conn_ref[a : a + 1, cut] - base, rows) for a in range(4)]
        moved = [pick(parts, hot[a][0], hot[a][1], rows) for a in range(4)]
        h = [[sum(moved[a][i] * grad[a][j] for a in range(4)) for j in range(3)] for i in range(3)]
        bulk = first * (h[0][0] + h[1][1] + h[2][2])
        stress = [[second * (h[i][j] + h[j][i]) for j in range(3)] for i in range(3)]
        for i in range(3):
            stress[i][i] = stress[i][i] + bulk
        for a in range(4):
            nodal = [sum(stress[i][j] * grad[a][j] for j in range(3)) for i in range(3)]
            total = total + spread(nodal, hot[a][0], hot[a][1])
    out_ref[...] = total.reshape(3, rows, LANES)


def call(kernel, shape, *args, **sizes):
    return pl.pallas_call(
        functools.partial(kernel, **sizes),
        out_shape=jax.ShapeDtypeStruct(shape, F32),
        compiler_params=pltpu.CompilerParams(vmem_limit_bytes=48 * 1024 * 1024),
    )(*args)


def shifted(shard, axis, by):
    size = lax.axis_size(axis)
    pairs = [(i, i + by) for i in range(size) if 0 <= i + by < size]
    return lax.ppermute(shard, axis, pairs)


def joined(field, own_rows, shared_rows):
    carried = shifted(field[:, own_rows:], "sub", 1)
    upper = shifted(field[:, :shared_rows], "sub", -1)
    return jnp.concatenate(
        [
            field[:, :shared_rows] + carried,
            field[:, shared_rows:own_rows],
            field[:, own_rows:] + upper,
        ],
        axis=1,
    )


def body(fine_res, node_map, connect, grads, moduli, mass):
    nodes = mass.shape[0]
    own = nodes // LANES
    shared = CI // LANES
    rows = own + shared
    sizes = dict(rows=rows, nodes=nodes)
    shape = (3, rows, LANES)
    weight = jnp.pad(mass.reshape(1, own, LANES), ((0, 0), (0, shared), (0, 0)))
    partial_rhs = call(restrict_kernel, shape, fine_res, node_map, **sizes)
    residual = joined(lax.psum(partial_rhs, "grp"), own, shared)
    gamma = alpha = answer = direction = image = None
    for step in range(ITERS):
        forces = call(force_kernel, shape, residual, connect, grads, moduli, **sizes)
        forces = forces + weight * residual
        inner = residual[:, :own]
        sums = lax.psum(jnp.stack([jnp.sum(inner * inner), jnp.sum(residual * forces)]), "sub")
        last = step + 1 == ITERS
        applied = None if last else joined(forces, own, shared)
        if step == 0:
            alpha = sums[0] / sums[1]
            direction = residual
            image = applied
            answer = alpha * direction
        else:
            beta = sums[0] / gamma
            alpha = sums[0] / (sums[1] - beta * sums[0] / alpha)
            direction = residual + beta * direction
            answer = answer + alpha * direction
            if not last:
                image = applied + beta * image
        gamma = sums[0]
        if not last:
            residual = residual - alpha * image
    return call(prolong_kernel, fine_res.shape, answer, node_map, **sizes)


def solution(mesh):
    in_specs = (
        P(None, ("grp", "sub")),
        P(None, ("grp", "sub")),
        P(None, "sub"),
        P(None, None, "sub"),
        P(None, "sub"),
        P("sub"),
    )
    out_specs = P(None, ("grp", "sub"))
    return jax.shard_map(body, mesh=mesh, in_specs=in_specs, out_specs=out_specs, check_vma=False)
```

profile of v0, /device:TPU:0, one launch (start us, length us, event | category | flops | bytes accessed | tf_op | source)
XLA Modules:
  0.0 129.4 jit_solution(8635618722386241972)
XLA Ops:
  0.0 0.8 copy-done.3
  0.8 0.8 copy-done.5
  1.6 1.2 shard_map.64
  2.9 13.3 %psum.28 = f32[3,24,128]{2,1,0:T(8,128)S(1)} all-reduce(f32[3,24,128]{2,1,0:T(8,128)S(1)} %shard_map.64), channel_id=1, replica_groups=mesh['grp'=4,'sub'=8] {'grp'}, use_global_device_ids=true, to_apply=%region_0.1 | all-reduce | flops 9216 | bytes 73728 | tf_op jit(solution)/shard_map/psum | solution.py:141
  16.2 3.4 %collective-permute-start = (f32[3,8,128]{2,1,0:T(8,128)S(1)}, f32[3,8,128]{2,1,0:T(8,128)S(1)}, u32[]{:S(2)}, u32[]{:S(2)}) collective-permute-start(f32[3,8,128]{2,1,0:T(8,128)S(1)} %get-tuple-element.22), channel_id=1, source_target_pairs={{0,1},{1,2},{2,3},{3,4},{4,5},{5,6},{6,7},{8,9},{9,10},{10,11},{11... | collective-permute-start | bytes 36872 | tf_op jit(solution)/shard_map/ppermute | solution.py:116
  19.6 1.3 collective-permute-start.1
  21.0 4.2 %collective-permute-done.1 = f32[3,8,128]{2,1,0:T(8,128)S(1)} collective-permute-done((f32[3,8,128]{2,1,0:T(8,128)S(1)}, f32[3,8,128]{2,1,0:T(8,128)S(1)}, u32[]{:S(2)}, u32[]{:S(2)}) %collective-permute-start.1) | collective-permute-done | bytes 12320 | tf_op jit(solution)/shard_map/ppermute | solution.py:116
  25.2 0.7 fusion.4
  26.7 5.0 %shard_map.65 = f32[3,24,128]{2,1,0:T(8,128)S(1)} custom-call(f32[3,24,128]{2,1,0:T(8,128)S(1)} %pad_maximum_fusion.field_ref, s32[4,4096]{1,0:T(4,128)S(1)} %copy-done.1, f32[3,3,4096]{2,1,0:T(4,128)S(1)} %copy-done, f32[2,4096]{1,0:T(2,128)S(1)} %copy-done.2), custom_call_target="tpu_custom_call" | custom-call | tf_op jit(solution)/shard_map/pallas_call | solution.py:106
  32.2 4.3 %collective-permute-start.2 = (f32[3,8,128]{2,1,0:T(8,128)S(1)}, f32[3,8,128]{2,1,0:T(8,128)S(1)}, u32[]{:S(2)}, u32[]{:S(2)}) collective-permute-start(f32[3,8,128]{2,1,0:T(8,128)S(1)} %get-tuple-element.17), channel_id=1, source_target_pairs={{0,1},{1,2},{2,3},{3,4},{4,5},{5,6},{6,7},{8,9},{9,10},{10,11},{11... | collective-permute-start | bytes 36872 | tf_op jit(solution)/shard_map/ppermute | solution.py:116
  36.6 1.4 %pad_maximum_fusion.2 = f32[2]{0:T(128)S(1)} fusion(f32[1]{0:T(128)} %bitcast.3, f32[1]{0:T(128)} %bitcast), kind=kLoop, calls=%fused_computation.19 | loop fusion | flops 2 | bytes 16 | tf_op jit(solution)/shard_map/stack | solution.py:147
  38.0 1.3 collective-permute-start.3
  39.3 20.4 %psum.29 = f32[2]{0:T(128)S(1)} all-reduce(f32[2]{0:T(128)S(1)} %pad_maximum_fusion.2), channel_id=1, replica_groups=mesh['grp'=4,'sub'=8] {'sub'}, use_global_device_ids=true, to_apply=%region_3.4 | all-reduce | flops 2 | bytes 16 | tf_op jit(solution)/shard_map/psum | solution.py:147
  61.7 5.0 %shard_map.66 = f32[3,24,128]{2,1,0:T(8,128)S(1)} custom-call(f32[3,24,128]{2,1,0:T(8,128)S(1)} %multiply_subtract_fusion.field_ref, s32[4,4096]{1,0:T(4,128)S(1)} %copy-done.1, f32[3,3,4096]{2,1,0:T(4,128)S(1)} %copy-done, f32[2,4096]{1,0:T(2,128)S(1)} %copy-done.2), custom_call_target="tpu_custom_call" | custom-call | tf_op jit(solution)/shard_map/pallas_call | solution.py:106
  67.9 2.1 %collective-permute-start.4 = (f32[3,8,128]{2,1,0:T(8,128)S(1)}, f32[3,8,128]{2,1,0:T(8,128)S(1)}, u32[]{:S(2)}, u32[]{:S(2)}) collective-permute-start(f32[3,8,128]{2,1,0:T(8,128)S(1)} %get-tuple-element.12), channel_id=1, source_target_pairs={{0,1},{1,2},{2,3},{3,4},{4,5},{5,6},{6,7},{8,9},{9,10},{10,11},{11... | collective-permute-start | bytes 36872 | tf_op jit(solution)/shard_map/ppermute | solution.py:116
  70.0 1.3 pad_maximum_fusion.3
  71.3 1.3 collective-permute-start.5
  72.6 19.9 %psum.30 = f32[2]{0:T(128)S(1)} all-reduce(f32[2]{0:T(128)S(1)} %pad_maximum_fusion.3), channel_id=1, replica_groups=mesh['grp'=4,'sub'=8] {'sub'}, use_global_device_ids=true, to_apply=%region_6.7 | all-reduce | flops 2 | bytes 16 | tf_op jit(solution)/shard_map/psum | solution.py:147
  97.6 5.0 %shard_map.67 = f32[3,24,128]{2,1,0:T(8,128)S(1)} custom-call(f32[3,24,128]{2,1,0:T(8,128)S(1)} %fusion.1.field_ref, s32[4,4096]{1,0:T(4,128)S(1)} %copy-done.1, f32[3,3,4096]{2,1,0:T(4,128)S(1)} %copy-done, f32[2,4096]{1,0:T(2,128)S(1)} %copy-done.2), custom_call_target="tpu_custom_call" | custom-call | tf_op jit(solution)/shard_map/pallas_call | solution.py:106
  102.6 0.7 fusion.2
  103.9 1.4 %pad_maximum_fusion.4 = f32[2]{0:T(128)S(1)} fusion(f32[1]{0:T(128)} %bitcast.11, f32[1]{0:T(128)} %bitcast.10), kind=kLoop, calls=%fused_computation.21 | loop fusion | flops 2 | bytes 16 | tf_op jit(solution)/shard_map/stack | solution.py:147
  105.3 17.1 %psum.31 = f32[2]{0:T(128)S(1)} all-reduce(f32[2]{0:T(128)S(1)} %pad_maximum_fusion.4), channel_id=1, replica_groups=mesh['grp'=4,'sub'=8] {'sub'}, use_global_device_ids=true, to_apply=%region_9.10 | all-reduce | flops 2 | bytes 16 | tf_op jit(solution)/shard_map/psum | solution.py:147
  127.0 0.7 copy-done.4
  127.7 1.7 %shard_map.68 = f32[3,4096]{1,0:T(4,128)} custom-call(f32[3,24,128]{2,1,0:T(8,128)S(1)} %multiply_add_fusion.field_ref, s32[2,4096]{1,0:T(2,128)S(1)} %copy-done.4), custom_call_target="tpu_custom_call" | custom-call | tf_op jit(solution)/shard_map/pallas_call | solution.py:106
  (34 shorter events, 5.2 us)
Async XLA Ops:
  0.0 0.8 copy-start.3
  0.8 0.8 copy-start.5
  1.6 19.3 %copy-start.6 = (f32[2048]{0:T(1024)S(1)}, f32[2048]{0:T(1024)}, u32[]{:S(2)}) copy-start(f32[2048]{0:T(1024)} %param.11) | copy-start | bytes 24580
  2.8 23.1 %copy-start = (f32[3,3,4096]{2,1,0:T(4,128)S(1)}, f32[3,3,4096]{2,1,0:T(4,128)}, u32[]{:S(2)}) copy-start(f32[3,3,4096]{2,1,0:T(4,128)} %grads_ref.5) | copy-start | bytes 442372
  16.2 4.8 %collective-permute-start = (f32[3,8,128]{2,1,0:T(8,128)S(1)}, f32[3,8,128]{2,1,0:T(8,128)S(1)}, u32[]{:S(2)}, u32[]{:S(2)}) collective-permute-start(f32[3,8,128]{2,1,0:T(8,128)S(1)} %get-tuple-element.22), channel_id=1, source_target_pairs={{0,1},{1,2},{2,3},{3,4},{4,5},{5,6},{6,7},{8,9},{9,10},{10,11},{11... | collective-permute-start | bytes 36872 | tf_op jit(solution)/shard_map/ppermute | solution.py:116
  19.6 5.6 %collective-permute-start.1 = (f32[3,8,128]{2,1,0:T(8,128)S(1)}, f32[3,8,128]{2,1,0:T(8,128)S(1)}, u32[]{:S(2)}, u32[]{:S(2)}) collective-permute-start(f32[3,8,128]{2,1,0:T(8,128)S(1)} %get-tuple-element.23), channel_id=1, source_target_pairs={{1,0},{2,1},{3,2},{4,3},{5,4},{6,5},{7,6},{9,8},{10,9},{11,10},{12... | collective-permute-start | bytes 36872 | tf_op jit(solution)/shard_map/ppermute | solution.py:116
  25.2 0.8 copy-start.1
  25.9 0.8 copy-start.2
  32.2 29.4 %collective-permute-start.2 = (f32[3,8,128]{2,1,0:T(8,128)S(1)}, f32[3,8,128]{2,1,0:T(8,128)S(1)}, u32[]{:S(2)}, u32[]{:S(2)}) collective-permute-start(f32[3,8,128]{2,1,0:T(8,128)S(1)} %get-tuple-element.17), channel_id=1, source_target_pairs={{0,1},{1,2},{2,3},{3,4},{4,5},{5,6},{6,7},{8,9},{9,10},{10,11},{11... | collective-permute-start | bytes 36872 | tf_op jit(solution)/shard_map/ppermute | solution.py:116
  38.0 23.7 %collective-permute-start.3 = (f32[3,8,128]{2,1,0:T(8,128)S(1)}, f32[3,8,128]{2,1,0:T(8,128)S(1)}, u32[]{:S(2)}, u32[]{:S(2)}) collective-permute-start(f32[3,8,128]{2,1,0:T(8,128)S(1)} %get-tuple-element.18), channel_id=1, source_target_pairs={{1,0},{2,1},{3,2},{4,3},{5,4},{6,5},{7,6},{9,8},{10,9},{11,10},{12... | collective-permute-start | bytes 36872 | tf_op jit(solution)/shard_map/ppermute | solution.py:116
  67.9 29.7 %collective-permute-start.4 = (f32[3,8,128]{2,1,0:T(8,128)S(1)}, f32[3,8,128]{2,1,0:T(8,128)S(1)}, u32[]{:S(2)}, u32[]{:S(2)}) collective-permute-start(f32[3,8,128]{2,1,0:T(8,128)S(1)} %get-tuple-element.12), channel_id=1, source_target_pairs={{0,1},{1,2},{2,3},{3,4},{4,5},{5,6},{6,7},{8,9},{9,10},{10,11},{11... | collective-permute-start | bytes 36872 | tf_op jit(solution)/shard_map/ppermute | solution.py:116
  71.3 26.3 %collective-permute-start.5 = (f32[3,8,128]{2,1,0:T(8,128)S(1)}, f32[3,8,128]{2,1,0:T(8,128)S(1)}, u32[]{:S(2)}, u32[]{:S(2)}) collective-permute-start(f32[3,8,128]{2,1,0:T(8,128)S(1)} %get-tuple-element.13), channel_id=1, source_target_pairs={{1,0},{2,1},{3,2},{4,3},{5,4},{6,5},{7,6},{9,8},{10,9},{11,10},{12... | collective-permute-start | bytes 36872 | tf_op jit(solution)/shard_map/ppermute | solution.py:116
  126.9 0.8 copy-start.4
where the time goes:
time: 130 us; the launch traced here: 129 us
  blocking collectives  70.8 us (54%)
  Pallas kernels  17.8 us (14%)
  starting transfers between devices  13.7 us (11%)
  between operations  9.94 us (8%)
  other arithmetic  7.98 us (6%)
  local copies, waits for them, and re-layouts  4.91 us (4%)
  waiting for transfers between devices  4.28 us (3%)
    psum x3, blocking collectives, body(): lax.psum(jnp.stack([jnp.sum(inner * inner), jnp.sum(residual * forces)]),...  57.5 us
    pallas_call x5, Pallas kernels, call(): pl.pallas_call(functools.partial(kernel, **sizes), out_shape=jax.ShapeDty...  17.8 us
    ppermute x6, starting transfers between devices, shifted(): return lax.ppermute(shard, axis, pairs)  13.7 us
    psum x1, blocking collectives, body(): residual = joined(lax.psum(partial_rhs, 'grp'), own, shared)  13.3 us
    ppermute x6, waiting for transfers between devices, shifted(): return lax.ppermute(shard, axis, pairs)  4.28 us
    another operation x3, other arithmetic, body(): jnp.stack([jnp.sum(inner * inner), jnp.sum(residual * forces)])  4.08 us
    unnamed x14, local copies, waits for them, and re-layouts  3.09 us
  transfers between devices with their start and end apart: 6, of which 2 were waited for; matrix products, arithmetic and copies ran while one was open for 3% of the time, Pallas kernels for 0%

commit v1 on v0

v1 whole, which is shorter than its diff:
```python
import functools

import jax
import jax.numpy as jnp
from jax import lax
from jax.experimental import pallas as pl
from jax.experimental.pallas import tpu as pltpu
from jax.sharding import PartitionSpec as P

CI = 1024
LANES = 128
TILE = 512
CORES = 2
F32 = jnp.float32
BF16 = jnp.bfloat16
NT = (((1,), (1,)), ((), ()))
MESH = pl.DeviceIdType.MESH


def split(value):
    high = value.astype(BF16)
    return high, (value - high.astype(F32)).astype(BF16)


def hots(index, rows):
    lane = index & (LANES - 1)
    row = index // LANES
    width = index.shape[1]
    lane_hot = jnp.where(lax.broadcasted_iota(jnp.int32, (LANES, width), 0) == lane, 1.0, 0.0).astype(BF16)
    row_hot = lax.broadcasted_iota(jnp.int32, (rows, width), 0) == row
    return lane_hot, row_hot


def pick(parts, lane_hot, row_hot, rows):
    got = jnp.dot(parts, lane_hot, preferred_element_type=F32)
    half = 3 * rows
    got = got[:half] + got[half:]
    return [
        jnp.sum(jnp.where(row_hot, got[d * rows : (d + 1) * rows], 0.0), axis=0, keepdims=True)
        for d in range(3)
    ]


def spread(values, lane_hot, row_hot):
    placed = []
    for value in values:
        placed.append(jnp.where(row_hot, value, 0.0))
    placed = jnp.concatenate(placed, axis=0)
    parts = jnp.concatenate(split(placed), axis=0)
    got = lax.dot_general(parts, lane_hot, NT, preferred_element_type=F32)
    half = got.shape[0] // 2
    return got[:half] + got[half:]


def field_parts(field):
    flat = field.reshape(-1, LANES)
    return jnp.concatenate(split(flat), axis=0)


def folded(row):
    return sum(row[:, at : at + LANES] for at in range(0, row.shape[1], LANES))


def down(value):
    return jnp.sum(value.reshape(-1, LANES), axis=0, keepdims=True)


def whole(row):
    return jnp.sum(row, axis=1, keepdims=True)


class Kernel:
    def __init__(self, refs, rows, nodes, own, shared, groups, columns):
        for name, ref in refs.items():
            setattr(self, name, ref)
        self.rows, self.nodes, self.own, self.shared = rows, nodes, own, shared
        self.groups, self.columns = groups, columns
        self.g = lax.axis_index("grp")
        self.s = lax.axis_index("sub")
        self.core = lax.rem(self.g, CORES)
        self.chip = self.g - self.core
        self.base = self.s * nodes
        self.sent = []
        self.count = 0

    def send(self, src, dst, grp, sub, when=None):
        at = self.count
        self.count += 1
        copy = pltpu.make_async_remote_copy(
            src_ref=src,
            dst_ref=dst,
            send_sem=self.send_sem.at[at],
            recv_sem=self.recv_sem.at[at],
            device_id={"grp": grp, "sub": sub},
            device_id_type=MESH,
        )
        self.guard(when, copy.start)
        self.sent.append((copy, when))
        return copy

    def guard(self, when, act):
        if when is None:
            act()
        else:
            pl.when(when)(act)

    def drain(self):
        for copy, when in self.sent:
            self.guard(when, copy.wait_send)

    def has_next(self):
        return self.s < self.columns - 1

    def has_prev(self):
        return self.s > 0

    def restrict(self):
        total = jnp.zeros((3 * self.rows, LANES), F32)
        for at in range(0, self.fine.shape[1], TILE):
            values = [0.5 * self.fine[d : d + 1, at : at + TILE] for d in range(3)]
            for k in range(2):
                lane_hot, row_hot = hots(self.nmap[k : k + 1, at : at + TILE] - self.base, self.rows)
                total = total + spread(values, lane_hot, row_hot)
        return total.reshape(3, self.rows, LANES)

    def prolong(self, field, out_ref):
        parts = field_parts(field)
        for at in range(0, self.fine.shape[1], TILE):
            both = []
            for k in range(2):
                lane_hot, row_hot = hots(self.nmap[k : k + 1, at : at + TILE] - self.base, self.rows)
                both.append(pick(parts, lane_hot, row_hot, self.rows))
            for d in range(3):
                out_ref[d : d + 1, at : at + TILE] = 0.5 * (both[0][d] + both[1][d])

    def apply(self, field, forces=True, energy=False):
        parts = field_parts(field)
        total = jnp.zeros((3 * self.rows, LANES), F32)
        power = jnp.zeros((1, LANES), F32)
        for at in range(0, self.conn.shape[1], TILE):
            cut = slice(at, at + TILE)
            grad = [[self.grads[i, a : a + 1, cut] for i in range(3)] for a in range(3)]
            grad.append([-(grad[0][i] + grad[1][i] + grad[2][i]) for i in range(3)])
            first = self.moduli[0:1, cut]
            second = self.moduli[1:2, cut]
            hot = [hots(self.conn[a : a + 1, cut] - self.base, self.rows) for a in range(4)]
            moved = [pick(parts, hot[a][0], hot[a][1], self.rows) for a in range(4)]
            h = [[sum(moved[a][i] * grad[a][j] for a in range(4)) for j in range(3)] for i in range(3)]
            bulk = first * (h[0][0] + h[1][1] + h[2][2])
            stress = [[second * (h[i][j] + h[j][i]) for j in range(3)] for i in range(3)]
            for i in range(3):
                stress[i][i] = stress[i][i] + bulk
            if energy:
                power = power + folded(sum(stress[i][j] * h[i][j] for i in range(3) for j in range(3)))
            if forces:
                for a in range(4):
                    nodal = [sum(stress[i][j] * grad[a][j] for j in range(3)) for i in range(3)]
                    total = total + spread(nodal, hot[a][0], hot[a][1])
        return total.reshape(3, self.rows, LANES), power

    def weighted(self, field):
        return 0.5 * self.mass[...][None] * field[:, : self.own]

    def exchange_forces(self, field, forces, phase):
        own, shared, rows = self.own, self.shared, self.rows
        f_ref = self.force.at[phase]
        f_ref[:, :own] = forces[:, :own] + self.weighted(field)
        f_ref[:, own:] = forces[:, own:]
        copies = []
        nxt, prv = self.has_next(), self.has_prev()
        for j in range(CORES):
            grp = self.chip + lax.rem(self.core + j, CORES)
            up = self.send(f_ref.at[:, pl.ds(own, shared)], self.h_prev.at[phase, j], grp, self.s + 1, nxt)
            copies.append((up, prv))
            dn = self.send(f_ref.at[:, pl.ds(0, shared)], self.h_next.at[phase, j], grp, self.s - 1, prv)
            copies.append((dn, nxt))
        grp = self.chip + 1 - self.core
        copies.append((self.send(f_ref, self.h_own.at[phase], grp, self.s), None))
        return copies

    def collect(self, copies):
        for copy, when in copies:
            self.guard(when, copy.wait_recv)

    def join(self, field, before, after):
        own, shared = self.own, self.shared
        return jnp.concatenate(
            [field[:, :shared] + before, field[:, shared:own], field[:, own:] + after], axis=1
        )

    def joined_forces(self, phase):
        both = self.force[phase] + self.h_own[phase]
        return self.join(
            both,
            self.h_prev[phase, 0] + self.h_prev[phase, 1],
            self.h_next[phase, 0] + self.h_next[phase, 1],
        )

    def share(self, buf, value, cores):
        slot = self.s * cores + (self.core if cores > 1 else 0)
        buf[slot] = value
        copies = []
        for k in range(self.columns):
            for j in range(cores):
                if k == 0 and j == 0:
                    continue
                sub = lax.rem(self.s + k, self.columns)
                grp = self.chip + lax.rem(self.core + j, CORES)
                copies.append((self.send(buf.at[slot], buf.at[slot], grp, sub), None))
        return copies

    def run(self):
        own, shared, rows, G = self.own, self.shared, self.rows, self.groups
        g, s = self.g, self.s
        nxt, prv = self.has_next(), self.has_prev()
        barrier = pltpu.get_barrier_semaphore()

        def greet(grp, sub, when=None):
            def act():
                pl.semaphore_signal(barrier, inc=1, device_id={"grp": grp, "sub": sub}, device_id_type=MESH)

            self.guard(when, act)

        for k in range(self.columns):
            for j in range(CORES):
                if k or j:
                    greet(self.chip + lax.rem(self.core + j, CORES), lax.rem(s + k, self.columns))
        for j in range(CORES, G):
            grp = lax.rem(self.chip + j, G)
            greet(grp, s)
            greet(grp, s + 1, nxt)
            greet(grp, s - 1, prv)
        half = self.conn.shape[1]
        at = pl.multiple_of(self.core * half, LANES)
        loads = []
        pairs = [
            (self.nmap_in, self.nmap),
            (self.fine_in, self.fine),
            (self.conn_in.at[:, pl.ds(at, half)], self.conn),
            (self.grads_in.at[:, :, pl.ds(at, half)], self.grads),
            (self.moduli_in.at[:, pl.ds(at, half)], self.moduli),
            (self.mass_in, self.mass),
        ]
        for i, (src, dst) in enumerate(pairs):
            copy = pltpu.make_async_copy(src, dst, self.load_sem.at[i])
            copy.start()
            loads.append(copy)

        @pl.when(jnp.logical_not(prv))
        def _():
            self.r_prev[...] = jnp.zeros_like(self.r_prev)
            self.h_prev[...] = jnp.zeros_like(self.h_prev)

        @pl.when(jnp.logical_not(nxt))
        def _():
            self.r_next[...] = jnp.zeros_like(self.r_next)
            self.h_next[...] = jnp.zeros_like(self.h_next)

        loads[0].wait()
        loads[1].wait()
        self.part[...] = self.restrict()
        far = G - CORES
        pl.semaphore_wait(
            barrier,
            self.columns * CORES - 1 + far + far * (nxt.astype(jnp.int32) + prv.astype(jnp.int32)),
        )
        copies = []
        for j in range(G):
            grp = lax.rem(g + j, G)
            up = self.send(self.part.at[:, pl.ds(own, shared)], self.r_prev.at[j], grp, s + 1, nxt)
            copies.append((up, prv))
            dn = self.send(self.part.at[:, pl.ds(0, shared)], self.r_next.at[j], grp, s - 1, prv)
            copies.append((dn, nxt))
            if j:
                copies.append((self.send(self.part, self.r_own.at[j - 1], grp, s), None))
        for copy in loads[2:]:
            copy.wait()
        self.collect(copies)
        r0 = self.join(
            self.part[...] + sum(self.r_own[j] for j in range(G - 1)),
            sum(self.r_prev[j] for j in range(G)),
            sum(self.r_next[j] for j in range(G)),
        )
        forces, _ = self.apply(r0)
        copies = self.exchange_forces(r0, forces, 0)
        self.prolong(r0, self.back.at[0])
        self.collect(copies)
        w0 = self.joined_forces(0)

        mine, image = r0[:, :own], w0[:, :own]
        first = self.share(
            self.sum1,
            jnp.concatenate([down(mine * mine), down(mine * image), down(image * image), down(image * image)], axis=0),
            1,
        )
        forces, power = self.apply(w0, energy=True)
        second = self.share(self.sum2, power + down(self.weighted(w0) * image), CORES)
        copies = self.exchange_forces(w0, forces, 1)
        self.collect(first)
        sums = sum(self.sum1[i] for i in range(self.columns))
        g0, m1, m2 = sums[0:1], sums[1:2], sums[2:3]
        gamma0, mu1, mu2 = whole(g0), whole(m1), whole(m2)
        alpha0 = gamma0 / mu1
        r1 = r0 - alpha0 * w0
        self.prolong(r1, self.back.at[1])
        self.collect(copies)
        q0 = self.joined_forces(1)
        self.collect(second)
        mu3 = whole(sum(self.sum2[i] for i in range(self.columns * CORES)))
        gamma1 = whole(g0 - 2.0 * alpha0 * m1 + (alpha0 * alpha0) * m2)
        delta1 = mu1 - 2.0 * alpha0 * mu2 + (alpha0 * alpha0) * mu3
        beta1 = gamma1 / gamma0
        alpha1 = gamma1 / (delta1 - beta1 * gamma1 / alpha0)
        r2 = r1 - alpha1 * ((w0 - alpha0 * q0) + beta1 * w0)
        _, power = self.apply(r2, forces=False, energy=True)
        mine = r2[:, :own]
        third = self.share(
            self.sum3,
            jnp.concatenate([0.5 * down(mine * mine), power + down(self.weighted(r2) * mine)], axis=0),
            CORES,
        )
        self.prolong(r2, self.back.at[2])
        self.collect(third)
        sums = sum(self.sum3[i] for i in range(self.columns * CORES))
        gamma2, delta2 = whole(sums[0:1]), whole(sums[1:2])
        beta2 = gamma2 / gamma1
        alpha2 = gamma2 / (delta2 - beta2 * gamma2 / alpha1)
        c1 = alpha1 + alpha2 * beta2
        c0 = alpha0 + beta1 * c1
        self.out[...] = c0 * self.back[0] + c1 * self.back[1] + alpha2 * self.back[2]
        self.drain()


NAMES = (
    "fine_in",
    "nmap_in",
    "conn_in",
    "grads_in",
    "moduli_in",
    "mass_in",
    "out",
    "fine",
    "nmap",
    "conn",
    "grads",
    "moduli",
    "mass",
    "part",
    "r_own",
    "r_prev",
    "r_next",
    "force",
    "h_own",
    "h_prev",
    "h_next",
    "sum1",
    "sum2",
    "sum3",
    "back",
    "load_sem",
    "send_sem",
    "recv_sem",
)


def kernel(*refs, **sizes):
    Kernel(dict(zip(NAMES, refs)), **sizes).run()


def body(groups, columns, fine_res, node_map, connect, grads, moduli, mass):
    nodes = mass.shape[0]
    own = nodes // LANES
    shared = CI // LANES
    rows = own + shared
    half = connect.shape[1] // CORES
    sends = 3 * groups - 1 + 2 * (2 * CORES + 1) + columns - 1 + 2 * (columns * CORES - 1)
    vmem = pltpu.VMEM
    halo = (3, shared, LANES)
    full = (3, rows, LANES)
    return pl.pallas_call(
        functools.partial(
            kernel, rows=rows, nodes=nodes, own=own, shared=shared, groups=groups, columns=columns
        ),
        out_shape=jax.ShapeDtypeStruct(fine_res.shape, F32),
        in_specs=[pl.BlockSpec(memory_space=pl.ANY)] * 6,
        out_specs=pl.BlockSpec(memory_space=vmem),
        scratch_shapes=[
            vmem(fine_res.shape, F32),
            vmem(node_map.shape, jnp.int32),
            vmem((4, half), jnp.int32),
            vmem((3, 3, half), F32),
            vmem((2, half), F32),
            vmem((own, LANES), F32),
            vmem(full, F32),
            vmem((groups - 1,) + full, F32),
            vmem((groups,) + halo, F32),
            vmem((groups,) + halo, F32),
            vmem((2,) + full, F32),
            vmem((2,) + full, F32),
            vmem((2, CORES) + halo, F32),
            vmem((2, CORES) + halo, F32),
            vmem((columns, 4, LANES), F32),
            vmem((columns * CORES, 1, LANES), F32),
            vmem((columns * CORES, 2, LANES), F32),
            vmem((3,) + fine_res.shape, F32),
            pltpu.SemaphoreType.DMA((6,)),
            pltpu.SemaphoreType.DMA((sends,)),
            pltpu.SemaphoreType.DMA((sends,)),
        ],
        compiler_params=pltpu.CompilerParams(
            collective_id=0, has_side_effects=True, vmem_limit_bytes=48 * 1024 * 1024
        ),
    )(fine_res, node_map, connect, grads, moduli, mass.reshape(own, LANES))


def solution(mesh):
    in_specs = (
        P(None, ("grp", "sub")),
        P(None, ("grp", "sub")),
        P(None, "sub"),
        P(None, None, "sub"),
        P(None, "sub"),
        P("sub"),
    )
    out_specs = P(None, ("grp", "sub"))
    return jax.shard_map(
        functools.partial(body, mesh.shape["grp"], mesh.shape["sub"]),
        mesh=mesh,
        in_specs=in_specs,
        out_specs=out_specs,
        check_vma=False,
    )
```

time: 130 us -> 34.8 us (0.27)
  blocking collectives: 70.8 us -> 0 us
  starting transfers between devices: 13.7 us -> 0 us
  Pallas kernels: 17.8 us -> 29 us
  between operations: 9.94 us -> 0.02 us
  other arithmetic: 7.98 us -> 0 us
  waiting for transfers between devices: 4.28 us -> 0 us
    psum x4 -> x0, blocking collectives: 70.8 us -> none  [the longest x3 57.5 us: body(): lax.psum(jnp.stack([jnp.sum(inner * inner), jnp.sum(residual * forces)]),...]
    ppermute x6 -> x0, starting transfers between devices: 13.7 us -> none  [shifted(): return lax.ppermute(shard, axis, pairs)]
    pallas_call x5 -> x1, Pallas kernels: 17.8 us -> 29 us  [body(): pl.pallas_call(functools.partial(kernel, rows=rows, nodes=nodes, own=own,...]
    ppermute x6 -> x0, waiting for transfers between devices: 4.28 us -> none  [shifted(): return lax.ppermute(shard, axis, pairs)]
    another operation x3 -> x0, other arithmetic: 4.08 us -> none  [body(): jnp.stack([jnp.sum(inner * inner), jnp.sum(residual * forces)])]
    reduce_sum x6 -> x0, other arithmetic: 3.83 us -> none  [the longest x3 2 us: body(): jnp.sum(inner * inner)]
    unnamed x14 -> x13, local copies, waits for them, and re-layouts: 3.09 us -> 5.45 us
    slice x6 -> x0, local copies, waits for them, and re-layouts: 1.81 us -> none  [the longest x2 1.21 us: body(): alpha = sums[0] / (sums[1] - beta * sums[0] / alpha)]
  transfers between devices with their start and end apart: 6 -> 0, of which waited for: 2 -> 0; matrix products, arithmetic and copies ran while one was open for 3% -> 0% of each run, Pallas kernels for 0% -> 0%
where the time goes in v1:
time: 34.8 us; the launch traced here: 34.4 us
  Pallas kernels  29 us (83%)
  local copies, waits for them, and re-layouts  5.45 us (16%)
    pallas_call x1, Pallas kernels, body(): pl.pallas_call(functools.partial(kernel, rows=rows, nodes=nodes, own=own,...  29 us
    unnamed x13, local copies, waits for them, and re-layouts  5.45 us

profile of v1, /device:TPU:0, one launch (start us, length us, event | category | flops | bytes accessed | tf_op | source)
XLA Modules:
  0.0 34.4 jit_solution(5362167979511975492)
XLA Ops:
  0.0 0.0 copy-start
  0.0 0.9 %copy-done = f32[3,3,4096]{2,1,0:T(4,128)S(1)} copy-done((f32[3,3,4096]{2,1,0:T(4,128)S(1)}, f32[3,3,4096]{2,1,0:T(4,128)}, u32[]{:S(2)}) %copy-start) | copy-done | bytes 147480
  0.9 0.0 copy-start.1
  0.9 0.8 %copy-done.1 = f32[3,4096]{1,0:T(4,128)S(1)} copy-done((f32[3,4096]{1,0:T(4,128)S(1)}, f32[3,4096]{1,0:T(4,128)}, u32[]{:S(2)}) %copy-start.1) | copy-done | bytes 49176
  1.8 0.0 copy-start.2
  1.8 0.8 %copy-done.2 = s32[4,4096]{1,0:T(4,128)S(1)} copy-done((s32[4,4096]{1,0:T(4,128)S(1)}, s32[4,4096]{1,0:T(4,128)}, u32[]{:S(2)}) %copy-start.2) | copy-done | bytes 65560
  2.6 0.0 copy-start.3
  2.6 0.8 %copy-done.3 = s32[2,4096]{1,0:T(2,128)S(1)} copy-done((s32[2,4096]{1,0:T(2,128)S(1)}, s32[2,4096]{1,0:T(2,128)}, u32[]{:S(2)}) %copy-start.3) | copy-done | bytes 32792
  3.4 0.0 copy-start.4
  3.4 0.8 %copy-done.4 = f32[2,4096]{1,0:T(2,128)S(1)} copy-done((f32[2,4096]{1,0:T(2,128)S(1)}, f32[2,4096]{1,0:T(2,128)}, u32[]{:S(2)}) %copy-start.4) | copy-done | bytes 32792
  4.1 0.0 copy-start.5
  4.1 0.7 %copy-done.5 = f32[2048]{0:T(1024)S(1)} copy-done((f32[2048]{0:T(1024)S(1)}, f32[2048]{0:T(1024)}, u32[]{:S(2)}) %copy-start.5) | copy-done | bytes 8216
  4.8 29.0 %shard_map.64 = f32[3,4096]{1,0:T(4,128)S(1)} custom-call(f32[3,4096]{1,0:T(4,128)S(1)} %copy-done.1, s32[2,4096]{1,0:T(2,128)S(1)} %copy-done.3, s32[4,4096]{1,0:T(4,128)S(1)} %copy-done.2, f32[3,3,4096]{2,1,0:T(4,128)S(1)} %copy-done, f32[2,4096]{1,0:T(2,128)S(1)} %copy-done.4, f32[16,128]{1,0:T(8,128)S(1)} %bitcast.1), custom_call_target="tpu_custom_call" | custom-call | tf_op jit(solution)/shard_map/pallas_call | solution.py:380
  33.8 0.6 %copy.8 = f32[3,4096]{1,0:T(4,128)} copy(f32[3,4096]{1,0:T(4,128)S(1)} %shard_map.64) | data formatting | bytes 98304
Async XLA Ops:
  0.0 0.9 %copy-start = (f32[3,3,4096]{2,1,0:T(4,128)S(1)}, f32[3,3,4096]{2,1,0:T(4,128)}, u32[]{:S(2)}) copy-start(f32[3,3,4096]{2,1,0:T(4,128)} %refs_3_.1) | copy-start | bytes 442372
  0.9 0.8 %copy-start.1 = (f32[3,4096]{1,0:T(4,128)S(1)}, f32[3,4096]{1,0:T(4,128)}, u32[]{:S(2)}) copy-start(f32[3,4096]{1,0:T(4,128)} %refs_0_.1) | copy-start | bytes 147460
  1.8 0.8 %copy-start.2 = (s32[4,4096]{1,0:T(4,128)S(1)}, s32[4,4096]{1,0:T(4,128)}, u32[]{:S(2)}) copy-start(s32[4,4096]{1,0:T(4,128)} %refs_2_.1) | copy-start | bytes 196612
  2.6 0.8 %copy-start.3 = (s32[2,4096]{1,0:T(2,128)S(1)}, s32[2,4096]{1,0:T(2,128)}, u32[]{:S(2)}) copy-start(s32[2,4096]{1,0:T(2,128)} %refs_1_.1) | copy-start | bytes 98308
  3.4 0.8 %copy-start.4 = (f32[2,4096]{1,0:T(2,128)S(1)}, f32[2,4096]{1,0:T(2,128)}, u32[]{:S(2)}) copy-start(f32[2,4096]{1,0:T(2,128)} %refs_4_.1) | copy-start | bytes 98308
  4.1 0.7 %copy-start.5 = (f32[2048]{0:T(1024)S(1)}, f32[2048]{0:T(1024)}, u32[]{:S(2)}) copy-start(f32[2048]{0:T(1024)} %param.11) | copy-start | bytes 24580

commit v2 on v1

--- a/solution.py
+++ b/solution.py
@@ -302,7 +302,6 @@
         gamma0, mu1, mu2 = whole(g0), whole(m1), whole(m2)
         alpha0 = gamma0 / mu1
         r1 = r0 - alpha0 * w0
-        self.prolong(r1, self.back.at[1])
         self.collect(copies)
         q0 = self.joined_forces(1)
         self.collect(second)
@@ -319,6 +318,7 @@
             jnp.concatenate([0.5 * down(mine * mine), power + down(self.weighted(r2) * mine)], axis=0),
             CORES,
         )
+        self.prolong(r1, self.back.at[1])
         self.prolong(r2, self.back.at[2])
         self.collect(third)
         sums = sum(self.sum3[i] for i in range(self.columns * CORES))
@@ -375,6 +375,7 @@
     half = connect.shape[1] // CORES
     sends = 3 * groups - 1 + 2 * (2 * CORES + 1) + columns - 1 + 2 * (columns * CORES - 1)
     vmem = pltpu.VMEM
+    arrays = (fine_res, node_map, connect, grads, moduli, mass.reshape(own, LANES))
     halo = (3, shared, LANES)
     full = (3, rows, LANES)
     return pl.pallas_call(
@@ -382,7 +383,7 @@
             kernel, rows=rows, nodes=nodes, own=own, shared=shared, groups=groups, columns=columns
         ),
         out_shape=jax.ShapeDtypeStruct(fine_res.shape, F32),
-        in_specs=[pl.BlockSpec(memory_space=pl.ANY)] * 6,
+        in_specs=[pl.BlockSpec(memory_space=pltpu.HBM)] * 6,
         out_specs=pl.BlockSpec(memory_space=vmem),
         scratch_shapes=[
             vmem(fine_res.shape, F32),
@@ -410,7 +411,7 @@
         compiler_params=pltpu.CompilerParams(
             collective_id=0, has_side_effects=True, vmem_limit_bytes=48 * 1024 * 1024
         ),
-    )(fine_res, node_map, connect, grads, moduli, mass.reshape(own, LANES))
+    )(*[pltpu.with_memory_space_constraint(x, pltpu.HBM) for x in arrays])
 
 
 def solution(mesh):

time: 34.8 us -> 29.8 us (0.86)
  local copies, waits for them, and re-layouts: 5.45 us -> 0.63 us
    unnamed x13 -> x1, local copies, waits for them, and re-layouts: 5.45 us -> 0.63 us
where the time goes in v2:
time: 29.8 us; the launch traced here: 29.6 us
  Pallas kernels  29 us (97%)
  local copies, waits for them, and re-layouts  0.63 us (2%)
    pallas_call x1, Pallas kernels, body(): pl.pallas_call(functools.partial(kernel, rows=rows, nodes=nodes, own=own,...  29 us
    unnamed x1, local copies, waits for them, and re-layouts  0.63 us

profile of v2, /device:TPU:0, one launch (start us, length us, event | category | flops | bytes accessed | tf_op | source)
XLA Modules:
  0.0 29.6 jit_solution(10513909343103320840)
XLA Ops:
  0.0 29.0 %shard_map.64 = f32[3,4096]{1,0:T(4,128)S(1)} custom-call(f32[3,4096]{1,0:T(4,128)} %refs_0_.1, s32[2,4096]{1,0:T(2,128)} %refs_1_.1, s32[4,4096]{1,0:T(4,128)} %refs_2_.1, f32[3,3,4096]{2,1,0:T(4,128)} %refs_3_.1, f32[2,4096]{1,0:T(2,128)} %refs_4_.1, f32[16,128]{1,0:T(8,128)} %bitcast.1), custom_call_target="tpu_custom_call" | custom-call | tf_op jit(solution)/shard_map/pallas_call | solution.py:381
  29.0 0.6 %copy.8 = f32[3,4096]{1,0:T(4,128)} copy(f32[3,4096]{1,0:T(4,128)S(1)} %shard_map.64) | data formatting | bytes 98304

commit v3 on v2

v3 whole, which is shorter than its diff:
```python
import functools

import jax
import jax.numpy as jnp
from jax import lax
from jax.experimental import pallas as pl
from jax.experimental.pallas import tpu as pltpu
from jax.sharding import PartitionSpec as P

CI = 1024
LANES = 128
TILE = 512
SUB = 8
CORES = 2
F32 = jnp.float32
BF16 = jnp.bfloat16
NT = (((1,), (1,)), ((), ()))
MESH = pl.DeviceIdType.MESH


def lane_hots(index):
    wide = lax.broadcasted_iota(jnp.int32, (LANES, index.shape[1]), 0)
    return jnp.where(wide == (index & (LANES - 1)), 1.0, 0.0).astype(BF16)


def turned_hots(index):
    square = (LANES, LANES)
    turned = jnp.transpose(jnp.broadcast_to(index & (LANES - 1), square))
    return jnp.where(lax.broadcasted_iota(jnp.int32, square, 1) == turned, 1.0, 0.0).astype(BF16)


def row_hots(index, rows):
    wide = lax.broadcasted_iota(jnp.int32, (2 * rows, index.shape[1]), 0)
    wide = wide // (2 * SUB) * SUB + (wide & (SUB - 1))
    return jnp.where(wide == index // LANES, 1.0, 0.0).astype(BF16)


def twice(value):
    high = value.astype(BF16).astype(F32)
    return high, value - high


def stacked(high, low):
    shape = (SUB, high.shape[1])
    both = jnp.concatenate([jnp.broadcast_to(high, shape), jnp.broadcast_to(low, shape)], axis=0)
    return both.astype(BF16)


def placed(values, row_hot):
    parts = []
    for value in values:
        for at in range(0, row_hot.shape[0], 2 * SUB):
            parts.append(row_hot[at : at + 2 * SUB] * value)
    return jnp.concatenate(parts, axis=0)


def merged(total, rows):
    total = total.reshape(3 * rows // SUB, 2, SUB, LANES)
    return (total[:, 0] + total[:, 1]).reshape(3, rows, LANES)


def gather(ref, lane, row):
    found = [jnp.zeros((SUB, LANES), F32) for _ in range(3)]
    for r in range(ref.shape[1]):
        here = row == r
        for d in range(3):
            line = jnp.broadcast_to(ref[d, r : r + 1, :], (SUB, LANES))
            found[d] = jnp.where(here, jnp.take_along_axis(line, lane, axis=1), found[d])
    return found


def down(value):
    return jnp.sum(value.reshape(-1, LANES), axis=0, keepdims=True)


def whole(row):
    return jnp.sum(row, axis=1, keepdims=True)


class Kernel:
    def __init__(self, refs, rows, nodes, own, shared, groups, columns):
        for name, ref in refs.items():
            setattr(self, name, ref)
        self.rows, self.nodes, self.own, self.shared = rows, nodes, own, shared
        self.groups, self.columns = groups, columns
        self.g = lax.axis_index("grp")
        self.s = lax.axis_index("sub")
        self.core = lax.rem(self.g, CORES)
        self.chip = self.g - self.core
        self.base = self.s * nodes
        self.sent = []
        self.count = 0

    def send(self, src, dst, grp, sub, when=None):
        at = self.count
        self.count += 1
        copy = pltpu.make_async_remote_copy(
            src_ref=src,
            dst_ref=dst,
            send_sem=self.send_sem.at[at],
            recv_sem=self.recv_sem.at[at],
            device_id={"grp": grp, "sub": sub},
            device_id_type=MESH,
        )
        self.guard(when, copy.start)
        self.sent.append((copy, when))
        return copy

    def guard(self, when, act):
        if when is None:
            act()
        else:
            pl.when(when)(act)

    def drain(self):
        for copy, when in self.sent:
            self.guard(when, copy.wait_send)
        self.sent = []

    def has_next(self):
        return self.s < self.columns - 1

    def has_prev(self):
        return self.s > 0

    def restrict(self):
        total = jnp.zeros((6 * self.rows, LANES), F32)
        for at in range(0, self.fine.shape[1], TILE):
            values = [stacked(*twice(0.5 * self.fine[d : d + 1, at : at + TILE])) for d in range(3)]
            for k in range(2):
                index = self.nmap[k : k + 1, at : at + TILE] - self.base
                left = placed(values, row_hots(index, self.rows))
                total = total + lax.dot_general(left, lane_hots(index), NT, preferred_element_type=F32)
        return merged(total, self.rows)

    def densify(self):
        for at in range(0, self.fine.shape[1], LANES):
            j = at // LANES
            for k in range(2):
                self.nmap_d[k, j : j + 1] = self.nmap[k : k + 1, at : at + LANES] - self.base
        for at in range(0, self.conn.shape[1], LANES):
            j, cut = at // LANES, slice(at, at + LANES)
            for a in range(4):
                self.conn_d[a, j : j + 1] = self.conn[a : a + 1, cut] - self.base
            for k in range(2):
                self.moduli_d[k, j : j + 1] = self.moduli[k : k + 1, cut]
            for i in range(3):
                line = [self.grads[i, a : a + 1, cut] for a in range(3)]
                for a in range(3):
                    self.grads_d[a, i, j : j + 1] = line[a]
                self.grads_d[3, i, j : j + 1] = -(line[0] + line[1] + line[2])

    def make_hots(self):
        width = self.conn.shape[1]
        for a in range(4):
            for at in range(0, width, TILE):
                index = self.conn[a : a + 1, at : at + TILE] - self.base
                for more in range(0, TILE, LANES):
                    start = a * width + at + more
                    self.lane_hot[start : start + LANES] = turned_hots(index[:, more : more + LANES])
                self.row_hot[:, a * width + at : a * width + at + TILE] = row_hots(index, self.rows)

    def prolong(self, field, out_ref):
        for j in range(0, self.nmap_d.shape[1], SUB):
            both = []
            for k in range(2):
                index = self.nmap_d[k, j : j + SUB]
                both.append(gather(field, index & (LANES - 1), index // LANES))
            for d in range(3):
                mean = 0.5 * (both[0][d] + both[1][d])
                for i in range(SUB):
                    out_ref[d : d + 1, (j + i) * LANES : (j + i + 1) * LANES] = mean[i : i + 1]

    def slopes(self, field, j, slot):
        cut = slice(j, j + SUB)
        grad = [[self.grads_d[a, i, cut] for i in range(3)] for a in range(4)]
        moved = []
        for a in range(4):
            index = self.conn_d[a, cut]
            moved.append(gather(field, index & (LANES - 1), index // LANES))
        h = [[sum(moved[a][i] * grad[a][k] for a in range(4)) for k in range(3)] for i in range(3)]
        for i in range(3):
            for k in range(3):
                self.slope[slot, i, k, cut] = h[i][k]
        return h, grad

    def stresses(self, h, j):
        first = self.moduli_d[0, j : j + SUB]
        second = self.moduli_d[1, j : j + SUB]
        bulk = first * (h[0][0] + h[1][1] + h[2][2])
        stress = [[second * (h[i][k] + h[k][i]) for k in range(3)] for i in range(3)]
        for i in range(3):
            stress[i][i] = stress[i][i] + bulk
        return stress, sum(stress[i][k] * h[i][k] for i in range(3) for k in range(3))

    def strains(self, field, j, slot):
        h, grad = self.slopes(field, j, slot)
        stress, power = self.stresses(h, j)
        nodal = []
        for a in range(4):
            nodal.append([twice(sum(stress[i][k] * grad[a][k] for k in range(3))) for i in range(3)])
        return power, nodal

    def blocks(self):
        return range(0, self.conn_d.shape[1], SUB)

    def energy(self, c1, c2):
        total = jnp.zeros((SUB, LANES), F32)
        for j in self.blocks():
            cut = slice(j, j + SUB)
            h = [
                [
                    self.slope[0, i, k, cut] - c1 * self.slope[1, i, k, cut] + c2 * self.slope[2, i, k, cut]
                    for k in range(3)
                ]
                for i in range(3)
            ]
            total = total + self.stresses(h, j)[1]
        return down(total)

    def hold(self, nodal, block):
        cut = slice(block, block + SUB)
        for a in range(4):
            for d in range(3):
                for k in range(2):
                    self.nodal[a, d, k, cut] = nodal[a][d][k]

    def spread(self, block, total):
        width = self.conn.shape[1]
        tile = TILE // LANES
        for a in range(4):
            for at in range(block, block + SUB, tile):
                values = []
                for d in range(3):
                    high, low = self.nodal.at[a, d, 0], self.nodal.at[a, d, 1]
                    pieces = [stacked(high[j : j + 1], low[j : j + 1]) for j in range(at, at + tile)]
                    values.append(jnp.concatenate(pieces, axis=1))
                cut = slice(a * width + at * LANES, a * width + at * LANES + TILE)
                left = placed(values, self.row_hot[:, cut])
                total = total + jnp.dot(left, self.lane_hot[cut], preferred_element_type=F32)
        return total

    def apply(self, field, slot, between=None):
        total = jnp.zeros((6 * self.rows, LANES), F32)
        power, held = None, None
        for block in self.blocks():
            more, nodal = self.strains(field, block, slot)
            power = more if power is None else power + more
            self.hold(nodal, block)
            if held is not None:
                total = self.spread(held, total)
            held = block
        extra = None if between is None else between(down(power))
        return merged(self.spread(held, total), self.rows), extra

    def weighted(self, field):
        return 0.5 * self.mass[...][None] * field[:, : self.own]

    def exchange_forces(self, field, forces, phase):
        own, shared, rows = self.own, self.shared, self.rows
        f_ref = self.force.at[phase]
        f_ref[:, :own] = forces[:, :own] + self.weighted(field)
        f_ref[:, own:] = forces[:, own:]
        copies = []
        nxt, prv = self.has_next(), self.has_prev()
        for j in range(CORES):
            grp = self.chip + lax.rem(self.core + j, CORES)
            up = self.send(f_ref.at[:, pl.ds(own, shared)], self.h_prev.at[phase, j], grp, self.s + 1, nxt)
            copies.append((up, prv))
            dn = self.send(f_ref.at[:, pl.ds(0, shared)], self.h_next.at[phase, j], grp, self.s - 1, prv)
            copies.append((dn, nxt))
        grp = self.chip + 1 - self.core
        copies.append((self.send(f_ref, self.h_own.at[phase], grp, self.s), None))
        return copies

    def collect(self, copies):
        for copy, when in copies:
            self.guard(when, copy.wait_recv)

    def join(self, field, before, after):
        own, shared = self.own, self.shared
        return jnp.concatenate(
            [field[:, :shared] + before, field[:, shared:own], field[:, own:] + after], axis=1
        )

    def joined_forces(self, phase):
        both = self.force[phase] + self.h_own[phase]
        return self.join(
            both,
            self.h_prev[phase, 0] + self.h_prev[phase, 1],
            self.h_next[phase, 0] + self.h_next[phase, 1],
        )

    def share(self, buf, value):
        slot = self.s * CORES + self.core
        buf[slot] = value
        copies = []
        for k in range(self.columns):
            for j in range(CORES):
                if k or j:
                    sub = lax.rem(self.s + k, self.columns)
                    grp = self.chip + lax.rem(self.core + j, CORES)
                    copies.append((self.send(buf.at[slot], buf.at[slot], grp, sub), None))
        return copies

    def total(self, buf):
        return sum(buf[i] for i in range(self.columns * CORES))

    def run(self):
        own, shared, rows, G = self.own, self.shared, self.rows, self.groups
        g, s = self.g, self.s
        nxt, prv = self.has_next(), self.has_prev()
        half = self.conn.shape[1]
        at = pl.multiple_of(self.core * half, LANES)
        loads = []
        pairs = [
            (self.nmap_in, self.nmap),
            (self.fine_in, self.fine),
            (self.conn_in.at[:, pl.ds(at, half)], self.conn),
            (self.grads_in.at[:, :, pl.ds(at, half)], self.grads),
            (self.moduli_in.at[:, pl.ds(at, half)], self.moduli),
            (self.mass_in, self.mass),
        ]
        for i, (src, dst) in enumerate(pairs):
            copy = pltpu.make_async_copy(src, dst, self.load_sem.at[i])
            copy.start()
            loads.append(copy)

        barrier = pltpu.get_barrier_semaphore()

        def greet(grp, sub, when=None):
            def act():
                pl.semaphore_signal(barrier, inc=1, device_id={"grp": grp, "sub": sub}, device_id_type=MESH)

            self.guard(when, act)

        ends = self.columns >= 8
        edge = jnp.logical_or(s < 2, s >= self.columns - 2)
        for k in range(self.columns):
            sub = lax.rem(s + k, self.columns)
            meets = None
            if ends and k:
                meets = jnp.logical_not(jnp.logical_and(edge, s + sub == self.columns - 1))
            for j in range(CORES):
                if k or j:
                    greet(self.chip + lax.rem(self.core + j, CORES), sub, meets)
        for j in range(CORES, G):
            grp = lax.rem(self.chip + j, G)
            greet(grp, s)
            greet(grp, s + 1, nxt)
            greet(grp, s - 1, prv)

        @pl.when(jnp.logical_not(prv))
        def _():
            self.r_prev[...] = jnp.zeros_like(self.r_prev)
            self.h_prev[...] = jnp.zeros_like(self.h_prev)

        @pl.when(jnp.logical_not(nxt))
        def _():
            self.r_next[...] = jnp.zeros_like(self.r_next)
            self.h_next[...] = jnp.zeros_like(self.h_next)

        loads[0].wait()
        loads[1].wait()
        self.part[...] = self.restrict()
        far = G - CORES
        missed = edge.astype(jnp.int32) if ends else 0
        pl.semaphore_wait(
            barrier,
            self.columns * CORES - 1 - CORES * missed + far + far * (nxt.astype(jnp.int32) + prv.astype(jnp.int32)),
        )
        copies = []
        for j in range(G):
            grp = lax.rem(g + j, G)
            up = self.send(self.part.at[:, pl.ds(own, shared)], self.r_prev.at[j], grp, s + 1, nxt)
            copies.append((up, prv))
            dn = self.send(self.part.at[:, pl.ds(0, shared)], self.r_next.at[j], grp, s - 1, prv)
            copies.append((dn, nxt))
            if j:
                copies.append((self.send(self.part, self.r_own.at[j - 1], grp, s), None))
        for copy in loads[2:]:
            copy.wait()
        self.densify()
        self.make_hots()
        self.collect(copies)
        r0 = self.join(
            self.part[...] + sum(self.r_own[j] for j in range(G - 1)),
            sum(self.r_prev[j] for j in range(G)),
            sum(self.r_next[j] for j in range(G)),
        )
        self.res[0] = r0
        forces, _ = self.apply(self.res.at[0], 0)
        copies = self.exchange_forces(r0, forces, 0)
        self.prolong(self.res.at[0], self.back.at[0])
        self.collect(copies)
        w0 = self.joined_forces(0)
        self.image[...] = w0
        mine, image = 0.5 * r0[:, :own], w0[:, :own]
        lines = [down(mine * r0[:, :own]), down(mine * image), down(0.5 * image * image)]
        weight = down(self.weighted(w0) * image)

        def early(power):
            return self.share(self.sum1, jnp.concatenate(lines + [power + weight], axis=0))

        forces, shares = self.apply(self.image, 1, early)
        copies = self.exchange_forces(w0, forces, 1)
        self.collect(copies)
        q0 = self.joined_forces(1)
        self.twin[...] = q0
        for j in self.blocks():
            self.slopes(self.twin, j, 2)
        self.collect(shares)
        sums = self.total(self.sum1)
        means = whole(sums)
        gamma0, mu1, mu2, mu3 = (means[i : i + 1] for i in range(4))
        alpha0 = gamma0 / mu1
        square = alpha0 * alpha0
        gamma1 = whole(sums[0:1] - 2.0 * alpha0 * sums[1:2] + square * sums[2:3])
        delta1 = mu1 - 2.0 * alpha0 * mu2 + square * mu3
        beta1 = gamma1 / gamma0
        alpha1 = gamma1 / (delta1 - beta1 * gamma1 / alpha0)
        a, b = alpha0 + alpha1 + alpha1 * beta1, alpha1 * alpha0
        r2 = r0 - a * w0 + b * q0
        mine = r2[:, :own]
        lines = [down(0.5 * mine * mine), down(self.weighted(r2) * mine) + self.energy(a, b)]
        shares = self.share(self.sum2, jnp.concatenate(lines, axis=0))
        self.res[1] = r0 - alpha0 * w0
        self.res[2] = r2
        self.prolong(self.res.at[1], self.back.at[1])
        self.prolong(self.res.at[2], self.back.at[2])
        self.drain()
        over_gamma, over_alpha = 1.0 / gamma1, 1.0 / alpha1
        self.collect(shares)
        means = whole(self.total(self.sum2))
        gamma2, delta2 = means[0:1], means[1:2]
        beta2 = gamma2 * over_gamma
        alpha2 = gamma2 / (delta2 - beta2 * (gamma2 * over_alpha))
        c1 = alpha1 + alpha2 * beta2
        c0 = alpha0 + beta1 * c1
        self.out[...] = c0 * self.back[0] + c1 * self.back[1] + alpha2 * self.back[2]


NAMES = (
    "fine_in",
    "nmap_in",
    "conn_in",
    "grads_in",
    "moduli_in",
    "mass_in",
    "out",
    "fine",
    "nmap",
    "conn",
    "grads",
    "moduli",
    "mass",
    "part",
    "r_own",
    "r_prev",
    "r_next",
    "force",
    "h_own",
    "h_prev",
    "h_next",
    "sum1",
    "sum2",
    "back",
    "res",
    "image",
    "twin",
    "slope",
    "nmap_d",
    "conn_d",
    "grads_d",
    "moduli_d",
    "nodal",
    "lane_hot",
    "row_hot",
    "load_sem",
    "send_sem",
    "recv_sem",
)


def kernel(*refs, **sizes):
    Kernel(dict(zip(NAMES, refs)), **sizes).run()


def body(groups, columns, fine_res, node_map, connect, grads, moduli, mass):
    nodes = mass.shape[0]
    own = nodes // LANES
    shared = CI // LANES
    rows = own + shared
    half = connect.shape[1] // CORES
    sends = 3 * groups - 1 + 2 * (2 * CORES + 1) + 2 * (columns * CORES - 1)
    vmem = pltpu.VMEM
    arrays = (fine_res, node_map, connect, grads, moduli, mass.reshape(own, LANES))
    halo = (3, shared, LANES)
    full = (3, rows, LANES)
    return pl.pallas_call(
        functools.partial(
            kernel, rows=rows, nodes=nodes, own=own, shared=shared, groups=groups, columns=columns
        ),
        out_shape=jax.ShapeDtypeStruct(fine_res.shape, F32),
        in_specs=[pl.BlockSpec(memory_space=pltpu.HBM)] * 6,
        out_specs=pl.BlockSpec(memory_space=vmem),
        scratch_shapes=[
            vmem(fine_res.shape, F32),
            vmem(node_map.shape, jnp.int32),
            vmem((4, half), jnp.int32),
            vmem((3, 3, half), F32),
            vmem((2, half), F32),
            vmem((own, LANES), F32),
            vmem(full, F32),
            vmem((groups - 1,) + full, F32),
            vmem((groups,) + halo, F32),
            vmem((groups,) + halo, F32),
            vmem((2,) + full, F32),
            vmem((2,) + full, F32),
            vmem((2, CORES) + halo, F32),
            vmem((2, CORES) + halo, F32),
            vmem((columns * CORES, 4, LANES), F32),
            vmem((columns * CORES, 2, LANES), F32),
            vmem((3,) + fine_res.shape, F32),
            vmem((3,) + full, F32),
            vmem(full, F32),
            vmem(full, F32),
            vmem((3, 3, 3, half // LANES, LANES), F32),
            vmem((2, node_map.shape[1] // LANES, LANES), jnp.int32),
            vmem((4, half // LANES, LANES), jnp.int32),
            vmem((4, 3, half // LANES, LANES), F32),
            vmem((2, half // LANES, LANES), F32),
            vmem((4, 3, 2, half // LANES, LANES), F32),
            vmem((4 * half, LANES), BF16),
            vmem((2 * rows, 4 * half), BF16),
            pltpu.SemaphoreType.DMA((6,)),
            pltpu.SemaphoreType.DMA((sends,)),
            pltpu.SemaphoreType.DMA((sends,)),
        ],
        compiler_params=pltpu.CompilerParams(
            collective_id=0, has_side_effects=True, vmem_limit_bytes=48 * 1024 * 1024
        ),
    )(*[pltpu.with_memory_space_constraint(x, pltpu.HBM) for x in arrays])


def solution(mesh):
    in_specs = (
        P(None, ("grp", "sub")),
        P(None, ("grp", "sub")),
        P(None, "sub"),
        P(None, None, "sub"),
        P(None, "sub"),
        P("sub"),
    )
    out_specs = P(None, ("grp", "sub"))
    return jax.shard_map(
        functools.partial(body, mesh.shape["grp"], mesh.shape["sub"]),
        mesh=mesh,
        in_specs=in_specs,
        out_specs=out_specs,
        check_vma=False,
    )
```

time: 29.8 us -> 26.8 us (0.90)
  Pallas kernels: 29 us -> 26 us
    pallas_call x1, Pallas kernels: 29 us -> 26 us  [body(): pl.pallas_call(functools.partial(kernel, rows=rows, nodes=nodes, own=own,...]
where the time goes in v3:
time: 26.8 us; the launch traced here: 26.7 us
  Pallas kernels  26 us (97%)
  local copies, waits for them, and re-layouts  0.63 us (2%)
    pallas_call x1, Pallas kernels, body(): pl.pallas_call(functools.partial(kernel, rows=rows, nodes=nodes, own=own,...  26 us
    unnamed x1, local copies, waits for them, and re-layouts  0.63 us

profile of v3, /device:TPU:0, one launch (start us, length us, event | category | flops | bytes accessed | tf_op | source)
XLA Modules:
  0.0 26.7 jit_solution(3399102863550100639)
XLA Ops:
  0.0 26.0 %shard_map.64 = f32[3,4096]{1,0:T(4,128)S(1)} custom-call(f32[3,4096]{1,0:T(4,128)} %refs_0_.1, s32[2,4096]{1,0:T(2,128)} %refs_1_.1, s32[4,4096]{1,0:T(4,128)} %refs_2_.1, f32[3,3,4096]{2,1,0:T(4,128)} %refs_3_.1, f32[2,4096]{1,0:T(2,128)} %refs_4_.1, f32[16,128]{1,0:T(8,128)} %bitcast.1), custom_call_target="tpu_custom_call" | custom-call | tf_op jit(solution)/shard_map/pallas_call | solution.py:500
  26.0 0.6 %copy.8 = f32[3,4096]{1,0:T(4,128)} copy(f32[3,4096]{1,0:T(4,128)S(1)} %shard_map.64) | data formatting | bytes 98304

commit v4 on v3

--- a/solution.py
+++ b/solution.py
@@ -88,10 +88,17 @@
         self.core = lax.rem(self.g, CORES)
         self.chip = self.g - self.core
         self.base = self.s * nodes
+        self.slot = self.s * CORES + self.core
+        self.all_blocks = self.conn_in.shape[1] // (SUB * LANES)
         self.sent = []
         self.count = 0
 
     def send(self, src, dst, grp, sub, when=None):
+        copy = self.prepare(src, dst, grp, sub, when)
+        self.guard(when, copy.start)
+        return copy
+
+    def prepare(self, src, dst, grp, sub, when=None):
         at = self.count
         self.count += 1
         copy = pltpu.make_async_remote_copy(
@@ -102,7 +109,6 @@
             device_id={"grp": grp, "sub": sub},
             device_id_type=MESH,
         )
-        self.guard(when, copy.start)
         self.sent.append((copy, when))
         return copy
 
@@ -201,12 +207,15 @@
             nodal.append([twice(sum(stress[i][k] * grad[a][k] for k in range(3))) for i in range(3)])
         return power, nodal
 
-    def blocks(self):
-        return range(0, self.conn_d.shape[1], SUB)
-
-    def energy(self, c1, c2):
+    def branches(self, act):
+        count = self.conn_d.shape[1] // SUB
+        few = self.all_blocks - count
+        for core, first in ((1, 0), (0, count - few)):
+            pl.when(self.core == core)(functools.partial(act, range(first * SUB, count * SUB, SUB)))
+
+    def energy(self, c1, c2, blocks):
         total = jnp.zeros((SUB, LANES), F32)
-        for j in self.blocks():
+        for j in blocks:
             cut = slice(j, j + SUB)
             h = [
                 [
@@ -240,27 +249,31 @@
                 total = total + jnp.dot(left, self.lane_hot[cut], preferred_element_type=F32)
         return total
 
-    def apply(self, field, slot, between=None):
+    def apply(self, field, slot, blocks, between=None):
         total = jnp.zeros((6 * self.rows, LANES), F32)
         power, held = None, None
-        for block in self.blocks():
+        for block in blocks:
             more, nodal = self.strains(field, block, slot)
             power = more if power is None else power + more
             self.hold(nodal, block)
             if held is not None:
                 total = self.spread(held, total)
             held = block
-        extra = None if between is None else between(down(power))
-        return merged(self.spread(held, total), self.rows), extra
+        if between is not None:
+            between(down(power))
+        return merged(self.spread(held, total), self.rows)
 
     def weighted(self, field):
         return 0.5 * self.mass[...][None] * field[:, : self.own]
 
-    def exchange_forces(self, field, forces, phase):
-        own, shared, rows = self.own, self.shared, self.rows
+    def keep(self, field, forces, phase):
+        own = self.own
+        self.force[phase, :, :own] = forces[:, :own] + self.weighted(field)
+        self.force[phase, :, own:] = forces[:, own:]
+
+    def exchange_forces(self, phase):
+        own, shared = self.own, self.shared
         f_ref = self.force.at[phase]
-        f_ref[:, :own] = forces[:, :own] + self.weighted(field)
-        f_ref[:, own:] = forces[:, own:]
         copies = []
         nxt, prv = self.has_next(), self.has_prev()
         for j in range(CORES):
@@ -291,16 +304,14 @@
             self.h_next[phase, 0] + self.h_next[phase, 1],
         )
 
-    def share(self, buf, value):
-        slot = self.s * CORES + self.core
-        buf[slot] = value
+    def share(self, buf):
         copies = []
         for k in range(self.columns):
             for j in range(CORES):
                 if k or j:
                     sub = lax.rem(self.s + k, self.columns)
                     grp = self.chip + lax.rem(self.core + j, CORES)
-                    copies.append((self.send(buf.at[slot], buf.at[slot], grp, sub), None))
+                    copies.append((self.prepare(buf.at[self.slot], buf.at[self.slot], grp, sub), None))
         return copies
 
     def total(self, buf):
@@ -311,7 +322,7 @@
         g, s = self.g, self.s
         nxt, prv = self.has_next(), self.has_prev()
         half = self.conn.shape[1]
-        at = pl.multiple_of(self.core * half, LANES)
+        at = pl.multiple_of((1 - self.core) * (self.conn_in.shape[1] - half), LANES)
         loads = []
         pairs = [
             (self.nmap_in, self.nmap),
@@ -369,46 +380,65 @@
             barrier,
             self.columns * CORES - 1 - CORES * missed + far + far * (nxt.astype(jnp.int32) + prv.astype(jnp.int32)),
         )
+        twin = self.send(self.part, self.r_own.at[0], self.chip + 1 - self.core, s)
         copies = []
-        for j in range(G):
-            grp = lax.rem(g + j, G)
+        for j in range(G - 1, -1, -1):
+            grp = lax.rem(self.chip + self.core + j, G)
             up = self.send(self.part.at[:, pl.ds(own, shared)], self.r_prev.at[j], grp, s + 1, nxt)
             copies.append((up, prv))
             dn = self.send(self.part.at[:, pl.ds(0, shared)], self.r_next.at[j], grp, s - 1, prv)
             copies.append((dn, nxt))
-            if j:
-                copies.append((self.send(self.part, self.r_own.at[j - 1], grp, s), None))
+        twin.wait_recv()
+        self.pair[...] = self.part[...] + self.r_own[0]
+        for j in range(1, G // CORES):
+            grp = lax.rem(g + CORES * j, G)
+            copies.append((self.send(self.pair, self.r_own.at[j], grp, s), None))
         for copy in loads[2:]:
             copy.wait()
         self.densify()
         self.make_hots()
         self.collect(copies)
         r0 = self.join(
-            self.part[...] + sum(self.r_own[j] for j in range(G - 1)),
+            self.pair[...] + sum(self.r_own[j] for j in range(1, G // CORES)),
             sum(self.r_prev[j] for j in range(G)),
             sum(self.r_next[j] for j in range(G)),
         )
         self.res[0] = r0
-        forces, _ = self.apply(self.res.at[0], 0)
-        copies = self.exchange_forces(r0, forces, 0)
+
+        def first(blocks):
+            self.keep(self.res[0], self.apply(self.res.at[0], 0, blocks), 0)
+
+        self.branches(first)
+        copies = self.exchange_forces(0)
         self.prolong(self.res.at[0], self.back.at[0])
         self.collect(copies)
         w0 = self.joined_forces(0)
         self.image[...] = w0
         mine, image = 0.5 * r0[:, :own], w0[:, :own]
         lines = [down(mine * r0[:, :own]), down(mine * image), down(0.5 * image * image)]
-        weight = down(self.weighted(w0) * image)
-
-        def early(power):
-            return self.share(self.sum1, jnp.concatenate(lines + [power + weight], axis=0))
-
-        forces, shares = self.apply(self.image, 1, early)
-        copies = self.exchange_forces(w0, forces, 1)
+        lines.append(down(self.weighted(w0) * image))
+        shares = self.share(self.sum1)
+        self.sum1[self.slot] = jnp.concatenate(lines, axis=0)
+
+        def second(blocks):
+            def early(power):
+                self.sum1[self.slot, 3:4] = self.sum1[self.slot, 3:4] + power
+                for copy, _ in shares:
+                    copy.start()
+
+            self.keep(self.image[...], self.apply(self.image, 1, blocks, early), 1)
+
+        self.branches(second)
+        copies = self.exchange_forces(1)
         self.collect(copies)
         q0 = self.joined_forces(1)
         self.twin[...] = q0
-        for j in self.blocks():
-            self.slopes(self.twin, j, 2)
+
+        def third(blocks):
+            for j in blocks:
+                self.slopes(self.twin, j, 2)
+
+        self.branches(third)
         self.collect(shares)
         sums = self.total(self.sum1)
         means = whole(sums)
@@ -422,8 +452,16 @@
         a, b = alpha0 + alpha1 + alpha1 * beta1, alpha1 * alpha0
         r2 = r0 - a * w0 + b * q0
         mine = r2[:, :own]
-        lines = [down(0.5 * mine * mine), down(self.weighted(r2) * mine) + self.energy(a, b)]
-        shares = self.share(self.sum2, jnp.concatenate(lines, axis=0))
+        lines = [down(0.5 * mine * mine), down(self.weighted(r2) * mine)]
+        shares = self.share(self.sum2)
+        self.sum2[self.slot] = jnp.concatenate(lines, axis=0)
+
+        def last(blocks):
+            self.sum2[self.slot, 1:2] = self.sum2[self.slot, 1:2] + self.energy(a, b, blocks)
+
+        self.branches(last)
+        for copy, _ in shares:
+            copy.start()
         self.res[1] = r0 - alpha0 * w0
         self.res[2] = r2
         self.prolong(self.res.at[1], self.back.at[1])
@@ -455,6 +493,7 @@
     "moduli",
     "mass",
     "part",
+    "pair",
     "r_own",
     "r_prev",
     "r_next",
@@ -491,8 +530,9 @@
     own = nodes // LANES
     shared = CI // LANES
     rows = own + shared
-    half = connect.shape[1] // CORES
-    sends = 3 * groups - 1 + 2 * (2 * CORES + 1) + 2 * (columns * CORES - 1)
+    blocks = connect.shape[1] // (SUB * LANES)
+    half = (blocks - max(1, blocks // 4)) * SUB * LANES
+    sends = 2 * groups + groups // CORES + 2 * (2 * CORES + 1) + 2 * (columns * CORES - 1)
     vmem = pltpu.VMEM
     arrays = (fine_res, node_map, connect, grads, moduli, mass.reshape(own, LANES))
     halo = (3, shared, LANES)
@@ -512,7 +552,8 @@
             vmem((2, half), F32),
             vmem((own, LANES), F32),
             vmem(full, F32),
-            vmem((groups - 1,) + full, F32),
+            vmem(full, F32),
+            vmem((groups // CORES,) + full, F32),
             vmem((groups,) + halo, F32),
             vmem((groups,) + halo, F32),
             vmem((2,) + full, F32),

time: 26.8 us -> 25.8 us (0.963)
  Pallas kernels: 26 us -> 25 us
    pallas_call x1, Pallas kernels: 26 us -> 25 us  [body(): pl.pallas_call(functools.partial(kernel, rows=rows, nodes=nodes, own=own,...]
where the time goes in v4:
time: 25.8 us; the launch traced here: 25.7 us
  Pallas kernels  25 us (97%)
  local copies, waits for them, and re-layouts  0.63 us (2%)
    pallas_call x1, Pallas kernels, body(): pl.pallas_call(functools.partial(kernel, rows=rows, nodes=nodes, own=own,...  25 us
    unnamed x1, local copies, waits for them, and re-layouts  0.63 us

profile of v4, /device:TPU:0, one launch (start us, length us, event | category | flops | bytes accessed | tf_op | source)
XLA Modules:
  0.0 25.7 jit_solution(81236309506167391)
XLA Ops:
  0.0 25.0 %shard_map.64 = f32[3,4096]{1,0:T(4,128)S(1)} custom-call(f32[3,4096]{1,0:T(4,128)} %refs_0_.1, s32[2,4096]{1,0:T(2,128)} %refs_1_.1, s32[4,4096]{1,0:T(4,128)} %refs_2_.1, f32[3,3,4096]{2,1,0:T(4,128)} %refs_3_.1, f32[2,4096]{1,0:T(2,128)} %refs_4_.1, f32[16,128]{1,0:T(8,128)} %bitcast.1), custom_call_target="tpu_custom_call" | custom-call | tf_op jit(solution)/shard_map/pallas_call | solution.py:540
  25.0 0.6 %copy.8 = f32[3,4096]{1,0:T(4,128)} copy(f32[3,4096]{1,0:T(4,128)S(1)} %shard_map.64) | data formatting | bytes 98304

commit v5 on v4

--- a/solution.py
+++ b/solution.py
@@ -346,12 +346,14 @@
             self.guard(when, act)
 
         ends = self.columns >= 8
-        edge = jnp.logical_or(s < 2, s >= self.columns - 2)
+        last = self.columns - 1
+        edge = jnp.logical_or(s < 2, s >= last - 1)
         for k in range(self.columns):
             sub = lax.rem(s + k, self.columns)
             meets = None
             if ends and k:
-                meets = jnp.logical_not(jnp.logical_and(edge, s + sub == self.columns - 1))
+                apart = jnp.logical_and(edge, jnp.logical_or(sub < 2, sub >= last - 1))
+                meets = jnp.logical_not(jnp.logical_and(apart, jnp.abs(s - sub) > 1))
             for j in range(CORES):
                 if k or j:
                     greet(self.chip + lax.rem(self.core + j, CORES), sub, meets)
@@ -375,7 +377,7 @@
         loads[1].wait()
         self.part[...] = self.restrict()
         far = G - CORES
-        missed = edge.astype(jnp.int32) if ends else 0
+        missed = 2 * edge.astype(jnp.int32) if ends else 0
         pl.semaphore_wait(
             barrier,
             self.columns * CORES - 1 - CORES * missed + far + far * (nxt.astype(jnp.int32) + prv.astype(jnp.int32)),
@@ -414,15 +416,15 @@
         self.collect(copies)
         w0 = self.joined_forces(0)
         self.image[...] = w0
-        mine, image = 0.5 * r0[:, :own], w0[:, :own]
-        lines = [down(mine * r0[:, :own]), down(mine * image), down(0.5 * image * image)]
-        lines.append(down(self.weighted(w0) * image))
         shares = self.share(self.sum1)
-        self.sum1[self.slot] = jnp.concatenate(lines, axis=0)
 
         def second(blocks):
             def early(power):
-                self.sum1[self.slot, 3:4] = self.sum1[self.slot, 3:4] + power
+                mine, image = self.res[0, :, :own], self.image[:, :own]
+                half = 0.5 * image
+                lines = [down(0.5 * mine * mine), down(mine * half), down(image * half)]
+                lines.append(down(self.weighted(image) * image) + power)
+                self.sum1[self.slot] = jnp.concatenate(lines, axis=0)
                 for copy, _ in shares:
                     copy.start()
 

time: 25.8 us -> 25.6 us (level)
  no operation moved by 1% of the time
where the time goes in v5:
time: 25.6 us; the launch traced here: 25.4 us
  Pallas kernels  24.8 us (97%)
  local copies, waits for them, and re-layouts  0.63 us (2%)
    pallas_call x1, Pallas kernels, body(): pl.pallas_call(functools.partial(kernel, rows=rows, nodes=nodes, own=own,...  24.8 us
    unnamed x1, local copies, waits for them, and re-layouts  0.63 us

profile of v5, /device:TPU:0, one launch (start us, length us, event | category | flops | bytes accessed | tf_op | source)
XLA Modules:
  0.0 25.4 jit_solution(1817836515122022135)
XLA Ops:
  0.0 24.8 %shard_map.64 = f32[3,4096]{1,0:T(4,128)S(1)} custom-call(f32[3,4096]{1,0:T(4,128)} %refs_0_.1, s32[2,4096]{1,0:T(2,128)} %refs_1_.1, s32[4,4096]{1,0:T(4,128)} %refs_2_.1, f32[3,3,4096]{2,1,0:T(4,128)} %refs_3_.1, f32[2,4096]{1,0:T(2,128)} %refs_4_.1, f32[16,128]{1,0:T(8,128)} %bitcast.1), custom_call_target="tpu_custom_call" | custom-call | tf_op jit(solution)/shard_map/pallas_call | solution.py:542
  24.8 0.6 %copy.8 = f32[3,4096]{1,0:T(4,128)} copy(f32[3,4096]{1,0:T(4,128)S(1)} %shard_map.64) | data formatting | bytes 98304
